TPU v7x, 32 devices: a whole 2x2x4 slice. The times are simulated.
32 devices in a mesh: param: 8 (over z, y), freq: 4 (over x, core).
Axes of the slice: x: 2, y: 2, z: 4, core: 2. Of those that a mesh axis runs over, the one named last changes fastest.
Arguments:
- kernel_hat: bfloat16 [2, 16, 600, 8192], P(None, 'freq', None, 'param'), may hold values from -0.25 to 0.25
- prior_gain: float32 [16, 8192], P('freq', 'param'), may hold values from 0.00045776367 to 0.018310547, as said below
- noise_var: float32 [600], replicated, may hold values from 0.5 to 2
- observed: float32 [8, 16, 600], P('param', 'freq'), may hold values from -6 to 6
Outputs:
- solution: float32 [8, 16, 600], P('param', 'freq')
- residual: float32 [8, 16, 600], P('param', 'freq')
Inputs may be any that keep to these rules, and one draw needn't show every extreme that they name: `prior_gain`: prior variances are positive.
All inputs are finite; a program needn't handle non-finite values.
Results may differ from a plain program's by a relative error of at most 0.0085.
Values may be sent and summed in bfloat16 or wider, within the bound.
A program may use at most 64 MiB of HBM per device.

v0:
```python
import math

import jax
import jax.numpy as jnp
from jax import lax
from jax.sharding import PartitionSpec as P

NT = 16
ITERS = 2


HIGHEST = lax.Precision.HIGHEST


def phase_tables(freq_first, freq_count, time_count, period):
    freq_ids = freq_first + lax.iota(jnp.int32, freq_count)
    time_ids = lax.iota(jnp.int32, time_count)
    phase_int = freq_ids[:, None] * time_ids[None, :] % period
    phase = phase_int.astype(jnp.float32) * (2.0 * math.pi / period)
    return (jnp.cos(phase), jnp.sin(phase))


def column_sum(left, right):
    return jnp.sum(left * right, axis=(1, 2))


def local(kernel_hat, prior_gain, noise_var, observed):
    slot_count = kernel_hat.shape[1]
    row_count = observed.shape[0]
    period = 2 * NT - 1
    freq_index = lax.axis_index("freq")
    real_part = kernel_hat[0]
    imag_part = kernel_hat[1]
    out_cos, out_sin = phase_tables(freq_index * slot_count, slot_count, NT, period)
    solution = jnp.zeros_like(observed)
    residual = observed
    direction = observed
    norm_now = lax.psum(column_sum(residual, residual), "freq")
    for sweep in range(ITERS):
        all_times = lax.all_gather(direction, "freq", axis=1, tiled=True)
        spec_real = jnp.einsum("kt,rts->rks", out_cos, all_times, precision=HIGHEST)
        spec_imag = -jnp.einsum("kt,rts->rks", out_sin, all_times, precision=HIGHEST)
        spectra = jnp.stack([spec_real, spec_imag], axis=1)
        apply_spectra = spectra.astype(jnp.bfloat16).reshape(row_count, -1)
        shard_piece = lax.all_gather(apply_spectra, "param", axis=0, tiled=True)
        blocks = shard_piece.reshape(shard_piece.shape[0], 2, slot_count, -1)
        upper = blocks[:, 0]
        lower = blocks[:, 1]
        coef_real = jnp.einsum(
            "rks,ksp->krp", upper, real_part, preferred_element_type=jnp.float32
        ) + jnp.einsum("rks,ksp->krp", lower, imag_part, preferred_element_type=jnp.float32)
        coef_imag = jnp.einsum(
            "rks,ksp->krp", lower, real_part, preferred_element_type=jnp.float32
        ) - jnp.einsum("rks,ksp->krp", upper, imag_part, preferred_element_type=jnp.float32)
        gathered = jnp.stack([coef_real, coef_imag], axis=0)
        apply_coeffs = (gathered * prior_gain[None, :, None, :]).astype(jnp.bfloat16)
        image_real = jnp.einsum(
            "ksp,krp->rks", real_part, apply_coeffs[0], preferred_element_type=jnp.float32
        ) - jnp.einsum(
            "ksp,krp->rks", imag_part, apply_coeffs[1], preferred_element_type=jnp.float32
        )
        image_imag = jnp.einsum(
            "ksp,krp->rks", real_part, apply_coeffs[1], preferred_element_type=jnp.float32
        ) + jnp.einsum(
            "ksp,krp->rks", imag_part, apply_coeffs[0], preferred_element_type=jnp.float32
        )
        image_hat = lax.psum_scatter(
            jnp.stack([image_real, image_imag], axis=1).reshape(
                lax.axis_size("param") * row_count, -1
            ),
            "param",
            scatter_dimension=0,
            tiled=True,
        )
        image_hat = image_hat.reshape(row_count, 2, slot_count, -1)
        partial_value = jnp.einsum(
            "rks,kt->rts", image_hat[:, 0], out_cos, precision=HIGHEST
        ) - jnp.einsum("rks,kt->rts", image_hat[:, 1], out_sin, precision=HIGHEST)
        inverse = lax.psum_scatter(partial_value, "freq", scatter_dimension=1, tiled=True)
        applied = noise_var[None, None, :] * direction + inverse
        curve_sum = lax.psum(column_sum(direction, applied), "freq")
        step_len = norm_now / curve_sum
        solution = solution + step_len[:, None, None] * direction
        residual = residual - step_len[:, None, None] * applied
        norm_next = lax.psum(column_sum(residual, residual), "freq")
        direction = residual + (norm_next / norm_now)[:, None, None] * direction
        norm_now = norm_next
    return (solution, residual)


def solution(mesh):
    return jax.shard_map(
        local,
        mesh=mesh,
        in_specs=(
            P(None, "freq", None, "param"),
            P("freq", "param"),
            P(),
            P("param", "freq", None),
        ),
        out_specs=(P("param", "freq", None), P("param", "freq", None)),
        check_vma=False,
    )
```

profile of v0, /device:TPU:0, one launch (start us, length us, event | category | flops | bytes accessed | tf_op | source)
XLA Modules:
  0.0 318.1 jit_solution(7416361258126682639)
XLA Ops:
  7.2 0.0 all-reduce.8.cloned.1.call-start
  7.2 0.7 copy.14
  7.9 6.2 %all_gather.12 = f32[1,16,600]{2,0,1:T(1,128)S(1)} all-gather(f32[1,4,600]{2,0,1:T(1,128)S(1)} %copy.14), channel_id=1, replica_groups=mesh['param'=8,'freq'=4] {'freq'}, dimensions={1}, use_global_device_ids=true | all-gather | bytes 48000 | tf_op jit(solution)/shard_map/all_gather | solution.py:40
  14.2 0.3 fusion.87
  14.4 0.3 fusion.84
  14.8 0.1 reshape.145
  14.9 31.4 %all-gather = bf16[8,1,4800]{2,1,0:T(2,128)(2,1)S(1)} all-gather(bf16[1,1,4800]{2,1,0:T(2,128)(2,1)S(1)} %reshape.145), channel_id=1, replica_groups=mesh['param'=8,'freq'=4] {'param'}, dimensions={0}, use_global_device_ids=true | all-gather | bytes 86400 | tf_op jit(solution)/shard_map/all_gather | solution.py:45
  46.3 0.4 reduce.4
  46.7 0.2 reshape.134
  46.9 0.0 copy-start
  47.0 3.4 %fusion.14 = f32[4,8,1024]{2,1,0:T(8,128)S(1)} fusion(bf16[2,4,600,1024]{3,2,1,0:T(8,128)(2,1)} %param.4, bf16[8,1,4,600]{3,2,1,0:T(4,128)(2,1)S(1)} %get-tuple-element.8), kind=kOutput, calls=%fused_computation.14 | convolution fusion | flops 39321600 | bytes 5084672 | tf_op jit(solution)/shard_map/rks,ksp->krp/dot_general | solution.py:51
  50.4 4.0 %fusion.12 = f32[4,8,1024]{2,1,0:T(8,128)S(1)} fusion(bf16[2,4,600,1024]{3,2,1,0:T(8,128)(2,1)} %param.4, bf16[8,1,4,600]{3,2,1,0:T(4,128)(2,1)S(1)} %get-tuple-element.9), kind=kOutput, calls=%fused_computation.12 | convolution fusion | flops 39321600 | bytes 5084672 | tf_op jit(solution)/shard_map/rks,ksp->krp/dot_general | solution.py:54
  54.4 1.1 fusion.35
  55.5 1.1 fusion.41
  56.6 0.0 copy-start.5
  56.6 0.0 copy-start.4
  56.7 0.0 copy-start.1
  56.7 0.0 copy-start.2
  56.7 1.4 fusion.8
  58.0 1.4 fusion.10
  59.4 1.4 fusion.65
  60.8 1.4 fusion.59
  62.3 0.8 reshape.135
  63.1 0.0 all-reduce.8.cloned.1.call-update
  63.1 0.0 all-reduce.10.cloned.1.call-start
  63.2 0.6 dynamic-slice.2
  63.8 0.6 dynamic-slice
  65.0 69.0 %all-reduce.8.cloned.1.call-done = f32[8,4800]{1,0:T(8,128)} async-done(((f32[8,4800]{1,0:T(8,128)}), f32[8,4800]{1,0:T(8,128)}) %all-reduce.8.cloned.1.call-update) | async-done | bytes 153616
  134.0 1.6 dynamic-slice_reduce_fusion.1
  135.7 0.1 reshape.136
  135.7 0.4 fusion.115
  136.1 0.4 fusion.81
  136.5 10.5 %all-reduce.1 = f32[1,16,600]{2,1,0:T(8,128)S(1)} all-reduce(f32[1,16,600]{2,1,0:T(8,128)S(1)} %fusion.81), channel_id=3, replica_groups=mesh['param'=8,'freq'=4] {'freq'}, use_global_device_ids=true, to_apply=%region_3.4.clone | all-reduce | flops 9600 | bytes 76800
  147.0 0.6 multiply_reduce_fusion.2
  147.7 7.1 %all-reduce.4 = (f32[1]{0:T(128)}, f32[1]{0:T(128)}) all-reduce(f32[1]{0:T(128)} %bitcast, f32[1]{0:T(128)} %bitcast.24), channel_id=1, replica_groups=mesh['param'=8,'freq'=4] {'freq'}, use_global_device_ids=true, to_apply=%region_1.2 | all-reduce | flops 2 | bytes 16 | tf_op jit(solution)/shard_map/psum | solution.py:38
  156.1 0.6 multiply_reduce_fusion.1
  156.8 6.7 %psum.30 = f32[1]{0:T(128)} all-reduce(f32[1]{0:T(128)} %bitcast.26), channel_id=1, replica_groups=mesh['param'=8,'freq'=4] {'freq'}, use_global_device_ids=true, to_apply=%region_7.8 | all-reduce | flops 1 | bytes 8 | tf_op jit(solution)/shard_map/psum | solution.py:85
  164.9 5.2 %all_gather.14 = f32[1,16,600]{2,0,1:T(1,128)S(1)} all-gather(f32[1,4,600]{2,0,1:T(1,128)S(1)} %copy.18), channel_id=1, replica_groups=mesh['param'=8,'freq'=4] {'freq'}, dimensions={1}, use_global_device_ids=true | all-gather | bytes 48000 | tf_op jit(solution)/shard_map/all_gather | solution.py:40
  170.1 0.3 fusion.86
  170.4 0.3 fusion.85
  170.7 0.1 reshape.147
  170.8 30.8 %all-gather.1 = bf16[8,1,4800]{2,1,0:T(2,128)(2,1)S(1)} all-gather(bf16[1,1,4800]{2,1,0:T(2,128)(2,1)S(1)} %reshape.147), channel_id=1, replica_groups=mesh['param'=8,'freq'=4] {'param'}, dimensions={0}, use_global_device_ids=true | all-gather | bytes 86400 | tf_op jit(solution)/shard_map/all_gather | solution.py:45
  201.5 0.4 reduce.6
  202.0 0.2 reshape.140
  202.2 0.0 slice-start.1
  202.2 3.4 %fusion.6 = f32[4,8,1024]{2,1,0:T(8,128)S(1)} fusion(bf16[2,4,600,1024]{3,2,1,0:T(8,128)(2,1)} %param.4, bf16[8,1,4,600]{3,2,1,0:T(4,128)(2,1)S(1)} %get-tuple-element.6), kind=kOutput, calls=%fused_computation.6 | convolution fusion | flops 39321600 | bytes 5084672 | tf_op jit(solution)/shard_map/rks,ksp->krp/dot_general | solution.py:51
  205.6 3.4 %fusion.4 = f32[4,8,1024]{2,1,0:T(8,128)S(1)} fusion(bf16[2,4,600,1024]{3,2,1,0:T(8,128)(2,1)} %param.4, bf16[8,1,4,600]{3,2,1,0:T(4,128)(2,1)S(1)} %get-tuple-element.7), kind=kOutput, calls=%fused_computation.4 | convolution fusion | flops 39321600 | bytes 5084672 | tf_op jit(solution)/shard_map/rks,ksp->krp/dot_general | solution.py:54
  209.0 3.3 %fusion.47 = f32[1,4,8,1024]{3,2,1,0:T(8,128)S(1)} fusion(f32[4,8,1024]{2,1,0:T(8,128)S(1)} %fusion.6, bf16[2,4,600,1024]{3,2,1,0:T(8,128)(2,1)} %param.4, bf16[8,1,4,600]{3,2,1,0:T(4,128)(2,1)S(1)} %get-tuple-element.7), kind=kOutput, calls=%fused_computation.37 | convolution fusion | flops 39354368 | bytes 5215744 | tf_op jit(solution)/shard_map/rks,ksp->krp/dot_general | solution.py:49
  212.3 0.9 fusion.53
  213.2 1.4 fusion
  214.5 1.4 fusion.2
  215.9 1.4 fusion.77
  217.3 1.4 fusion.71
  218.8 0.8 reshape.141
  219.6 0.0 all-reduce.10.cloned.1.call-update
  219.6 69.1 %all-reduce.10.cloned.1.call-done = f32[8,4800]{1,0:T(8,128)} async-done(((f32[8,4800]{1,0:T(8,128)}), f32[8,4800]{1,0:T(8,128)}) %all-reduce.10.cloned.1.call-update) | async-done | bytes 153616
  288.7 1.6 dynamic-slice_reduce_fusion
  290.3 0.1 reshape.142
  290.4 0.4 fusion.114
  290.8 0.4 fusion.80
  291.2 10.5 %all-reduce.3 = f32[1,16,600]{2,1,0:T(8,128)S(1)} all-reduce(f32[1,16,600]{2,1,0:T(8,128)S(1)} %fusion.80), channel_id=5, replica_groups=mesh['param'=8,'freq'=4] {'freq'}, use_global_device_ids=true, to_apply=%region_9.10.clone | all-reduce | flops 9600 | bytes 76800
  301.7 0.6 multiply_reduce_fusion
  302.3 7.0 %psum.31 = f32[1]{0:T(128)} all-reduce(f32[1]{0:T(128)} %bitcast.47), channel_id=1, replica_groups=mesh['param'=8,'freq'=4] {'freq'}, use_global_device_ids=true, to_apply=%region_11.12 | all-reduce | flops 1 | bytes 8 | tf_op jit(solution)/shard_map/psum | solution.py:81
  310.7 0.6 multiply_subtract_fusion
  (26 shorter events, 0.3 us)
Async XLA Ops:
  7.2 126.9 %all-reduce.8.cloned.1.call-start = ((), (), s32[]{:S(2)}) async-start(), calls=%async_computation | async-start | bytes 311296
  46.9 7.5 %copy-start = (bf16[2,4,600,1024]{3,2,1,0:T(8,128)(2,1)S(1)}, bf16[2,4,600,1024]{3,2,1,0:T(8,128)(2,1)}, u32[]{:S(2)}) copy-start(bf16[2,4,600,1024]{3,2,1,0:T(8,128)(2,1)} %param.4) | copy-start | bytes 29491204
  46.9 9.7 %copy-start.3 = (f32[4,1024]{1,0:T(4,128)S(1)}, f32[4,1024]{1,0:T(4,128)}, u32[]{:S(2)}) copy-start(f32[4,1024]{1,0:T(4,128)} %param.5) | copy-start | bytes 49156
  56.6 6.5 %copy-start.5 = (u32[32]{0:T(128)S(1)}, u32[32]{0:T(128)}, u32[]{:S(2)}) copy-start(u32[32]{0:T(128)} %constant.29) | copy-start | bytes 388
  56.6 7.1 %copy-start.4 = (u32[32]{0:T(128)S(1)}, u32[32]{0:T(128)}, u32[]{:S(2)}) copy-start(u32[32]{0:T(128)} %constant.25) | copy-start | bytes 388
  56.7 90.4 %copy-start.1 = (f32[1,4,600]{2,1,0:T(4,128)S(1)}, f32[1,4,600]{2,1,0:T(4,128)}, u32[]{:S(2)}) copy-start(f32[1,4,600]{2,1,0:T(4,128)} %param.7) | copy-start | bytes 28804
  56.7 90.4 %copy-start.2 = (f32[600]{0:T(1024)S(1)}, f32[600]{0:T(1024)}, u32[]{:S(2)}) copy-start(f32[600]{0:T(1024)} %param.6) | copy-start | bytes 7204
  62.2 150.0 %slice-start = ((s8[9830400]{0:T(1024)(128)(4,1)}), s8[1441792]{0:T(1024)(128)(4,1)S(1)}, s32[]{:S(2)}) async-start(s8[9830400]{0:T(1024)(128)(4,1)} %bitcast.189), calls=%async_computation.2 | async-start | bytes 2883584
  63.1 225.6 %all-reduce.10.cloned.1.call-start = ((), (), s32[]{:S(2)}) async-start(), calls=%async_computation.1 | async-start | bytes 311296
  202.2 10.1 %slice-start.1 = ((s8[9830400]{0:T(1024)(128)(4,1)}), s8[4194304]{0:T(1024)(128)(4,1)S(1)}, s32[]{:S(2)}) async-start(s8[9830400]{0:T(1024)(128)(4,1)} %bitcast.189), calls=%async_computation.3 | async-start | bytes 8388608
  205.6 6.7 %slice-start.2 = ((s8[9830400]{0:T(1024)(128)(4,1)}), s8[4194304]{0:T(1024)(128)(4,1)S(1)}, s32[]{:S(2)}) async-start(s8[9830400]{0:T(1024)(128)(4,1)} %bitcast.189), calls=%async_computation.4 | async-start | bytes 8388608
Sparse Core Ops, SparseCore 0:
  63.2 70.7 all-reduce.7
  219.7 68.9 all-reduce.9
where the time goes:
time: 319 us; the launch traced here: 318 us
  waiting for transfers between devices  138 us (43%)
  blocking collectives  115 us (36%)
  matrix products  34.2 us (11%)
  between operations  19.1 us (6%)
  local copies, waits for them, and re-layouts  7.62 us (2%)
  other arithmetic  3.49 us (1%)
    unnamed x4, waiting for transfers between devices  138 us
    all_gather x2, blocking collectives, local(): shard_piece = lax.all_gather(apply_spectra, 'param', axis=0, tiled=True)  62.2 us
    unnamed x2, blocking collectives  21 us
    all_gather x2, blocking collectives, local(): all_times = lax.all_gather(direction, 'freq', axis=1, tiled=True)  11.4 us
    dot_general x2, matrix products, local(): jnp.einsum('rks,ksp->krp', upper, imag_part, preferred_element_type=jnp.f...  7.43 us
    psum x1, blocking collectives, local(): norm_now = lax.psum(column_sum(residual, residual), 'freq')  7.1 us
    psum x1, blocking collectives, local(): curve_sum = lax.psum(column_sum(direction, applied), 'freq')  7.02 us
    dot_general x2, matrix products, local(): jnp.einsum('rks,ksp->krp', lower, imag_part, preferred_element_type=jnp.f...  6.81 us
  transfers between devices with their start and end apart: 2, of which 2 were waited for; matrix products, arithmetic and copies ran while one was open for 0% of the time, Pallas kernels for 0%

commit v1 on v0

v1 whole, which is shorter than its diff:
```python
import functools
import math

import jax
import jax.numpy as jnp
import numpy as np
from jax import lax
from jax.experimental import pallas as pl
from jax.experimental.pallas import tpu as pltpu
from jax.sharding import PartitionSpec as P

ITERS = 2
LANES = 128
F32 = jnp.float32
BF16 = jnp.bfloat16
HIGHEST = lax.Precision.HIGHEST


def phase_tables(freqs, times):
    period = 2 * times - 1
    ids = np.arange(freqs)[:, None] * np.arange(times)[None, :] % period
    phase = ids.astype(np.float32) * np.float32(2.0 * math.pi / period)
    return np.cos(phase).astype(np.float32), np.sin(phase).astype(np.float32)


def kernel(
    n_param,
    n_freq,
    obs_ref,
    kernel_ref,
    gain_ref,
    noise_ref,
    fwd_ref,
    inv_ref,
    sol_ref,
    res_ref,
    k_buf,
    obs_buf,
    sp_send,
    sp_buf,
    sp_wide,
    img_send,
    img_buf,
    row_send,
    row_buf,
    k_sem,
    obs_sems,
    sp_sems,
    img_sems,
    row_sems,
):
    _, slots, sensors, _ = kernel_ref.shape
    padded = k_buf.shape[2]
    tiles = padded // LANES
    comps = 2 * slots
    me_p = lax.axis_index("param")
    me_f = lax.axis_index("freq")

    loads = [
        pltpu.make_async_copy(
            kernel_ref.at[:, k], k_buf.at[:, k, pl.ds(0, sensors)], k_sem.at[k]
        )
        for k in range(slots)
    ]
    for load in loads:
        load.start()
    k_buf[:, :, sensors:, :] = jnp.zeros(
        (2, slots, padded - sensors, k_buf.shape[3]), BF16
    )

    barrier = pltpu.get_barrier_semaphore()
    for d in range(1, n_freq):
        pl.semaphore_signal(
            barrier, inc=1, device_id={"freq": lax.rem(me_f + d, n_freq)}
        )
    for d in range(1, n_param):
        pl.semaphore_signal(
            barrier, inc=1, device_id={"param": lax.rem(me_p + d, n_param)}
        )
    pl.semaphore_wait(barrier, n_freq + n_param - 2)

    def exchange(axis, me, n, source, target, sems):
        sent = []
        for d in range(1, n):
            peer = lax.rem(me + d, n)
            copy = pltpu.make_async_remote_copy(
                src_ref=source(peer),
                dst_ref=target.at[me],
                send_sem=sems.at[0, peer],
                recv_sem=sems.at[1, me],
                device_id={axis: peer},
            )
            copy.start()
            sent.append(copy)

        def arrive():
            for d in range(1, n):
                peer = lax.rem(me + n - d, n)
                pltpu.make_async_remote_copy(
                    src_ref=source(peer),
                    dst_ref=target.at[peer],
                    send_sem=sems.at[0, peer],
                    recv_sem=sems.at[1, peer],
                    device_id={axis: peer},
                ).wait_recv()

        def left():
            for copy in sent:
                copy.wait_send()

        return arrive, left

    pending = []
    block = obs_ref.shape[0]
    obs_buf[me_f] = obs_ref[...]
    arrive, left = exchange(
        "freq", me_f, n_freq, lambda peer: obs_ref, obs_buf, obs_sems
    )
    pending.append(left)
    arrive()
    tail = jnp.zeros((block * n_freq, padded - sensors), F32)
    field = jnp.concatenate([obs_buf[j] for j in range(n_freq)], axis=0)
    field = jnp.concatenate([field, tail], axis=1)
    noise = jnp.concatenate([noise_ref[...], tail[:1]], axis=1)

    fwd = fwd_ref[me_f]
    inv = inv_ref[...]
    solution = jnp.zeros_like(field)
    residual = field
    direction = field
    norm_now = jnp.sum(residual * residual, keepdims=True)
    for sweep in range(ITERS):
        spectra = jnp.dot(fwd, direction, precision=HIGHEST, preferred_element_type=F32)
        spectra = spectra.astype(BF16)
        sp_send[sweep] = spectra
        arrive, left = exchange(
            "param",
            me_p,
            n_param,
            lambda peer: sp_send.at[sweep],
            sp_buf.at[sweep],
            sp_sems.at[sweep],
        )
        pending.append(left)
        sp_buf[sweep, me_p] = spectra
        arrive()
        for r in range(n_param):
            wide = sp_buf[sweep, r].astype(F32)
            for l in range(tiles):
                sp_wide[l, r * comps : (r + 1) * comps, :] = wide[
                    :, l * LANES : (l + 1) * LANES
                ]

        def rows_of(comp):
            return jnp.concatenate(
                [
                    sp_wide[l, pl.ds(comp, n_param, stride=comps), :]
                    for l in range(tiles)
                ],
                axis=1,
            )

        for k in range(slots):
            if sweep == 0:
                loads[k].wait()
            upper, lower = rows_of(k), rows_of(slots + k)
            first = jnp.concatenate([upper, lower], axis=0).astype(BF16)
            second = jnp.concatenate([lower, -upper], axis=0).astype(BF16)
            coef = jnp.dot(
                first, k_buf[0, k], preferred_element_type=F32
            ) + jnp.dot(second, k_buf[1, k], preferred_element_type=F32)
            coef = coef * gain_ref[k : k + 1, :]
            turned = jnp.concatenate([-coef[n_param:], coef[:n_param]], axis=0)
            contract = (((1,), (1,)), ((), ()))
            image = lax.dot_general(
                coef.astype(BF16), k_buf[0, k], contract, preferred_element_type=F32
            ) + lax.dot_general(
                turned.astype(BF16), k_buf[1, k], contract, preferred_element_type=F32
            )
            for c in range(2):
                for l in range(tiles):
                    img_send[
                        sweep, l, pl.ds(c * slots + k, n_param, stride=comps), :
                    ] = image[
                        c * n_param : (c + 1) * n_param, l * LANES : (l + 1) * LANES
                    ]

        def part(peer):
            start = pl.multiple_of(peer * comps, comps)
            return img_send.at[sweep, :, pl.ds(start, comps), :]

        arrive, left = exchange(
            "param", me_p, n_param, part, img_buf.at[sweep], img_sems.at[sweep]
        )
        pending.append(left)
        img_buf[sweep, me_p] = img_send[
            sweep, :, pl.ds(pl.multiple_of(me_p * comps, comps), comps), :
        ]
        arrive()
        total = img_buf[sweep, 0]
        for r in range(1, n_param):
            total = total + img_buf[sweep, r]
        row_send[sweep] = total
        arrive, left = exchange(
            "freq",
            me_f,
            n_freq,
            lambda peer: row_send.at[sweep],
            row_buf.at[sweep],
            row_sems.at[sweep],
        )
        pending.append(left)
        row_buf[sweep, me_f] = total
        arrive()
        image = jnp.concatenate(
            [
                jnp.concatenate([row_buf[sweep, j, l] for l in range(tiles)], axis=1)
                for j in range(n_freq)
            ],
            axis=0,
        )
        inverse = jnp.dot(inv, image, precision=HIGHEST, preferred_element_type=F32)
        applied = noise * direction + inverse
        step_len = norm_now / jnp.sum(direction * applied, keepdims=True)
        solution = solution + step_len * direction
        residual = residual - step_len * applied
        if sweep + 1 < ITERS:
            norm_next = jnp.sum(residual * residual, keepdims=True)
            direction = residual + (norm_next / norm_now) * direction
            norm_now = norm_next

    for out_ref, value in ((sol_ref, solution), (res_ref, residual)):
        own = value[:block]
        for j in range(1, n_freq):
            own = jnp.where(me_f == j, value[j * block : (j + 1) * block], own)
        out_ref[...] = own[:, :sensors]
    for left in pending:
        left()


def solution(mesh):
    n_param, n_freq = mesh.shape["param"], mesh.shape["freq"]

    def local(kernel_hat, prior_gain, noise_var, observed):
        _, slots, sensors, params = kernel_hat.shape
        rows, block, _ = observed.shape
        assert rows == 1
        times = block * n_freq
        padded = -(-sensors // LANES) * LANES
        tiles = padded // LANES
        comps = 2 * slots
        cos, sin = phase_tables(slots * n_freq, times)
        pieces = np.stack([cos, -sin]).reshape(2, n_freq, slots, times)
        forward = pieces.transpose(1, 0, 2, 3).reshape(n_freq, comps, times)
        inverse = forward.reshape(n_freq * comps, times).T.copy()
        vmem = pl.BlockSpec(memory_space=pltpu.VMEM)
        out = jax.ShapeDtypeStruct((block, sensors), F32)
        dma = pltpu.SemaphoreType.DMA
        results = pl.pallas_call(
            functools.partial(kernel, n_param, n_freq),
            out_shape=(out, out),
            in_specs=[vmem, pl.BlockSpec(memory_space=pl.ANY)] + [vmem] * 4,
            out_specs=(vmem, vmem),
            scratch_shapes=[
                pltpu.VMEM((2, slots, padded, params), BF16),
                pltpu.VMEM((n_freq, block, sensors), F32),
                pltpu.VMEM((ITERS, comps, padded), BF16),
                pltpu.VMEM((ITERS, n_param, comps, padded), BF16),
                pltpu.VMEM((tiles, n_param * comps, LANES), F32),
                pltpu.VMEM((ITERS, tiles, n_param * comps, LANES), F32),
                pltpu.VMEM((ITERS, n_param, tiles, comps, LANES), F32),
                pltpu.VMEM((ITERS, tiles, comps, LANES), F32),
                pltpu.VMEM((ITERS, n_freq, tiles, comps, LANES), F32),
                dma((slots,)),
                dma((2, n_freq)),
                dma((ITERS, 2, n_param)),
                dma((ITERS, 2, n_param)),
                dma((ITERS, 2, n_freq)),
            ],
            compiler_params=pltpu.CompilerParams(
                collective_id=0,
                has_side_effects=True,
                vmem_limit_bytes=48 * 1024 * 1024,
            ),
        )(
            observed.reshape(block, sensors),
            kernel_hat,
            prior_gain,
            noise_var.reshape(1, sensors),
            jnp.asarray(forward),
            jnp.asarray(inverse),
        )
        return tuple(value.reshape(observed.shape) for value in results)

    return jax.shard_map(
        local,
        mesh=mesh,
        in_specs=(
            P(None, "freq", None, "param"),
            P("freq", "param"),
            P(),
            P("param", "freq", None),
        ),
        out_specs=(P("param", "freq", None), P("param", "freq", None)),
        check_vma=False,
    )
```

time: 319 us -> 51.3 us (0.16)
  waiting for transfers between devices: 138 us -> 0 us
  blocking collectives: 115 us -> 0 us
  Pallas kernels: 0 us -> 45.5 us
  matrix products: 34.2 us -> 0 us
  between operations: 19.1 us -> 0.64 us
  other arithmetic: 3.49 us -> 0 us
    unnamed x4 -> x0, waiting for transfers between devices: 138 us -> none
    all_gather x4 -> x0, blocking collectives: 73.6 us -> none  [the longest x2 62.2 us: local(): shard_piece = lax.all_gather(apply_spectra, 'param', axis=0, tiled=True)]
    pallas_call x0 -> x1, Pallas kernels: none -> 45.5 us  [local(): pl.pallas_call(functools.partial(kernel, n_param, n_freq), out_shape=(out...]
    dot_general x24 -> x0, matrix products: 34.2 us -> none  [the longest x2 7.43 us: local(): jnp.einsum('rks,ksp->krp', upper, imag_part, preferred_element_type=jnp.f...]
    unnamed x2 -> x0, blocking collectives: 21 us -> none
    psum x3 -> x0, blocking collectives: 20.8 us -> none  [the longest x1 7.1 us: local(): norm_now = lax.psum(column_sum(residual, residual), 'freq')]
  transfers between devices with their start and end apart: 2 -> 0, of which waited for: 2 -> 0; matrix products, arithmetic and copies ran while one was open for 0% -> 0% of each run, Pallas kernels for 0% -> 0%
where the time goes in v1:
time: 51.3 us; the launch traced here: 50.8 us
  Pallas kernels  45.5 us (89%)
  local copies, waits for them, and re-layouts  4.72 us (9%)
  between operations  0.64 us (1%)
    pallas_call x1, Pallas kernels, local(): pl.pallas_call(functools.partial(kernel, n_param, n_freq), out_shape=(out...  45.5 us
    unnamed x10, local copies, waits for them, and re-layouts  4.03 us

profile of v1, /device:TPU:0, one launch (start us, length us, event | category | flops | bytes accessed | tf_op | source)
XLA Modules:
  0.0 50.8 jit_solution(2127173397170895112)
XLA Ops:
  0.6 0.7 %reshape.17.noise_ref = f32[1,600]{1,0:T(1,128)S(1)} reshape(f32[600]{0:T(1024)} %param.8) | data formatting | bytes 4800 | tf_op jit(solution)/shard_map/reshape | solution.py:289
  1.3 0.0 copy-start
  1.3 0.7 %copy-done = f32[4,1024]{1,0:T(4,128)S(1)} copy-done((f32[4,1024]{1,0:T(4,128)S(1)}, f32[4,1024]{1,0:T(4,128)}, u32[]{:S(2)}) %copy-start) | copy-done | bytes 16408
  2.0 0.0 copy-start.1
  2.0 0.7 %copy-done.1 = f32[4,8,16]{2,1,0:T(8,128)S(1)} copy-done((f32[4,8,16]{2,1,0:T(8,128)S(1)}, f32[4,8,16]{2,1,0:T(8,128)}, u32[]{:S(2)}) %copy-start.1) | copy-done | bytes 2072
  2.8 0.0 copy-start.2
  2.8 0.7 %copy-done.2 = f32[1,4,600]{2,1,0:T(4,128)S(1)} copy-done((f32[1,4,600]{2,1,0:T(4,128)S(1)}, f32[1,4,600]{2,1,0:T(4,128)}, u32[]{:S(2)}) %copy-start.2) | copy-done | bytes 9624
  3.5 0.0 copy-start.3
  3.5 0.7 %copy-done.3 = f32[16,32]{1,0:T(8,128)S(1)} copy-done((f32[16,32]{1,0:T(8,128)S(1)}, f32[16,32]{1,0:T(8,128)}, u32[]{:S(2)}) %copy-start.3) | copy-done | bytes 2072
  4.2 45.5 %shard_map.77 = (f32[4,600]{1,0:T(4,128)S(1)}, f32[4,600]{1,0:T(4,128)S(1)}) custom-call(f32[4,600]{1,0:T(4,128)S(1)} %bitcast.3, bf16[2,4,600,1024]{3,2,1,0:T(8,128)(2,1)} %kernel_ref.1, f32[4,1024]{1,0:T(4,128)S(1)} %copy-done, f32[1,600]{1,0:T(1,128)S(1)} %reshape.17.noise_ref, f32[4,8,16]{2,1,0:T(8,128)S(1)} %copy-done.1, f32[16,32]{1,0:T(8,128)S(1)} %copy-done.3), custom_call_target="tpu_custom_call" | custom-call | tf_op jit(solution)/shard_map/pallas_call | solution.py:259
  49.6 0.6 %copy.10 = f32[1,4,600]{2,1,0:T(4,128)} copy(f32[1,4,600]{2,1,0:T(4,128)S(1)} %bitcast.5) | data formatting | bytes 19200
  50.2 0.6 %copy.11 = f32[1,4,600]{2,1,0:T(4,128)} copy(f32[1,4,600]{2,1,0:T(4,128)S(1)} %bitcast.4) | data formatting | bytes 19200
Async XLA Ops:
  1.3 0.7 %copy-start = (f32[4,1024]{1,0:T(4,128)S(1)}, f32[4,1024]{1,0:T(4,128)}, u32[]{:S(2)}) copy-start(f32[4,1024]{1,0:T(4,128)} %gain_ref.1) | copy-start | bytes 49156
  2.0 0.7 %copy-start.1 = (f32[4,8,16]{2,1,0:T(8,128)S(1)}, f32[4,8,16]{2,1,0:T(8,128)}, u32[]{:S(2)}) copy-start(f32[4,8,16]{2,1,0:T(8,128)} %constant.4.clone.fwd_ref) | copy-start | bytes 6148
  2.8 0.7 %copy-start.2 = (f32[1,4,600]{2,1,0:T(4,128)S(1)}, f32[1,4,600]{2,1,0:T(4,128)}, u32[]{:S(2)}) copy-start(f32[1,4,600]{2,1,0:T(4,128)} %param.9) | copy-start | bytes 28804
  3.5 0.7 %copy-start.3 = (f32[16,32]{1,0:T(8,128)S(1)}, f32[16,32]{1,0:T(8,128)}, u32[]{:S(2)}) copy-start(f32[16,32]{1,0:T(8,128)} %constant.5.clone.inv_ref) | copy-start | bytes 6148

commit v2 on v1

v2 whole, which is shorter than its diff:
```python
import functools
import math

import jax
import jax.numpy as jnp
import numpy as np
from jax import lax
from jax.experimental import pallas as pl
from jax.experimental.pallas import tpu as pltpu
from jax.sharding import PartitionSpec as P

ITERS = 2
LANES = 128
CHUNK = 5
F32 = jnp.float32
BF16 = jnp.bfloat16
HIGHEST = lax.Precision.HIGHEST


def phase_tables(freqs, times):
    period = 2 * times - 1
    ids = np.arange(freqs)[:, None] * np.arange(times)[None, :] % period
    phase = ids.astype(np.float32) * np.float32(2.0 * math.pi / period)
    return np.cos(phase).astype(np.float32), np.sin(phase).astype(np.float32)


def sensor_chunks(padded):
    tiles = padded // LANES
    return [(t, min(CHUNK, tiles - t)) for t in range(0, tiles, CHUNK)]


def kernel(
    n_param,
    n_freq,
    obs_ref,
    kernel_ref,
    gain_ref,
    noise_ref,
    fwd_ref,
    inv_ref,
    sol_ref,
    res_ref,
    k_buf,
    obs_buf,
    gain_buf,
    noise_buf,
    fwd_buf,
    inv_buf,
    fwd_wide,
    inv_wide,
    sp_send,
    sp_buf,
    sp_wide,
    img_send,
    img_buf,
    row_send,
    row_buf,
    k_sem,
    small_sem,
    obs_sems,
    sp_sems,
    img_sems,
    row_sems,
):
    _, slots, sensors, _ = kernel_ref.shape
    padded = k_buf.shape[2]
    tiles = padded // LANES
    chunks = sensor_chunks(padded)
    comps = 2 * slots
    me_p = lax.axis_index("param")
    me_f = lax.axis_index("freq")

    barrier = pltpu.get_barrier_semaphore()
    for d in range(1, n_freq):
        pl.semaphore_signal(
            barrier, inc=1, device_id={"freq": lax.rem(me_f + d, n_freq)}
        )
    for d in range(1, n_param):
        pl.semaphore_signal(
            barrier, inc=1, device_id={"param": lax.rem(me_p + d, n_param)}
        )
    small = [
        pltpu.make_async_copy(obs_ref.at[0], obs_buf.at[me_f], small_sem.at[0]),
        pltpu.make_async_copy(gain_ref, gain_buf, small_sem.at[1]),
        pltpu.make_async_copy(noise_ref, noise_buf, small_sem.at[2]),
        pltpu.make_async_copy(fwd_ref.at[me_f], fwd_buf, small_sem.at[3]),
        pltpu.make_async_copy(inv_ref, inv_buf, small_sem.at[4]),
    ]
    loads = []
    for i, (first, count) in enumerate(chunks):
        rows = pl.ds(first * LANES, min(count * LANES, sensors - first * LANES))
        loads.append(
            pltpu.make_async_copy(
                kernel_ref.at[:, :, rows], k_buf.at[:, :, rows], k_sem.at[i]
            )
        )
    for load in small + loads:
        load.start()
    k_buf[:, :, sensors:, :] = jnp.zeros(
        (2, slots, padded - sensors, k_buf.shape[3]), BF16
    )

    pl.semaphore_wait(barrier, n_freq + n_param - 2)

    def exchange(axis, me, n, source, target, sems):
        sent = []
        for d in range(1, n):
            peer = lax.rem(me + d, n)
            copy = pltpu.make_async_remote_copy(
                src_ref=source(peer),
                dst_ref=target(me),
                send_sem=sems.at[0, peer],
                recv_sem=sems.at[1, me],
                device_id={axis: peer},
            )
            copy.start()
            sent.append(copy)

        inbound = []
        for d in range(1, n):
            peer = lax.rem(me + n - d, n)
            inbound.append(
                pltpu.make_async_remote_copy(
                    src_ref=source(peer),
                    dst_ref=target(peer),
                    send_sem=sems.at[0, peer],
                    recv_sem=sems.at[1, peer],
                    device_id={axis: peer},
                )
            )

        def arrive():
            for copy in inbound:
                copy.wait_recv()

        def left():
            for copy in sent:
                copy.wait_send()

        return arrive, left

    pending = []
    block = obs_ref.shape[1]
    small[0].wait()
    arrive, left = exchange(
        "freq",
        me_f,
        n_freq,
        lambda peer: obs_buf.at[me_f],
        lambda slot: obs_buf.at[slot],
        obs_sems,
    )
    pending.append(left)
    for copy in small[1:]:
        copy.wait()
    for table, wide in ((fwd_buf, fwd_wide), (inv_buf, inv_wide)):
        held = table[...]
        for m in range(wide.shape[0]):
            wide[m] = jnp.broadcast_to(held[:, m : m + 1], wide.shape[1:])

    def weighted(wide, rows):
        sums = [wide[m] * row for m, row in enumerate(rows)]
        while len(sums) > 1:
            sums = [sum(sums[m : m + 2]) for m in range(0, len(sums), 2)]
        return sums[0]

    arrive()
    tail = jnp.zeros((block * n_freq, padded - sensors), F32)
    field = jnp.concatenate([obs_buf[j] for j in range(n_freq)], axis=0)
    field = jnp.concatenate([field, tail], axis=1)
    noise = jnp.concatenate([noise_buf[...].reshape(1, sensors), tail[:1]], axis=1)

    solution = jnp.zeros_like(field)
    residual = field
    direction = field
    norm_now = jnp.sum(residual * residual, keepdims=True)
    for sweep in range(ITERS):
        waits = []
        for i, (head, count) in enumerate(chunks):
            lanes = pl.ds(head * LANES, count * LANES)
            stretch = direction[:, head * LANES : (head + count) * LANES]
            spectra = jnp.concatenate(
                [
                    weighted(
                        fwd_wide,
                        [
                            stretch[t : t + 1, l * LANES : (l + 1) * LANES]
                            for t in range(block * n_freq)
                        ],
                    )
                    for l in range(count)
                ],
                axis=1,
            ).astype(BF16)
            sp_send[sweep, :, lanes] = spectra
            arrive, left = exchange(
                "param",
                me_p,
                n_param,
                lambda peer: sp_send.at[sweep, :, lanes],
                lambda slot: sp_buf.at[sweep, slot, :, lanes],
                sp_sems.at[sweep, i],
            )
            sp_buf[sweep, me_p, :, lanes] = spectra
            waits.append(arrive)
            pending.append(left)

        coefs = [0.0] * slots
        for i, (head, count) in enumerate(chunks):
            lanes = pl.ds(head * LANES, count * LANES)
            waits[i]()
            if sweep == 0:
                loads[i].wait()
            for r in range(n_param):
                wide = sp_buf[sweep, r, :, lanes].astype(F32)
                for l in range(count):
                    sp_wide[head + l, r * comps : (r + 1) * comps, :] = wide[
                        :, l * LANES : (l + 1) * LANES
                    ]

            def rows_of(comp):
                return jnp.concatenate(
                    [
                        sp_wide[head + l, pl.ds(comp, n_param, stride=comps), :]
                        for l in range(count)
                    ],
                    axis=1,
                )

            for k in range(slots):
                upper, lower = rows_of(k), rows_of(slots + k)
                ahead = jnp.concatenate([upper, lower], axis=0).astype(BF16)
                turned = jnp.concatenate([lower, -upper], axis=0).astype(BF16)
                coefs[k] = (
                    coefs[k]
                    + jnp.dot(ahead, k_buf[0, k, lanes], preferred_element_type=F32)
                    + jnp.dot(turned, k_buf[1, k, lanes], preferred_element_type=F32)
                )

        pairs = []
        for k in range(slots):
            coef = coefs[k] * gain_buf[k : k + 1, :]
            turned = jnp.concatenate([-coef[n_param:], coef[:n_param]], axis=0)
            pairs.append((coef.astype(BF16), turned.astype(BF16)))
        contract = (((1,), (1,)), ((), ()))
        waits = []
        for i, (head, count) in enumerate(chunks):
            lanes = pl.ds(head * LANES, count * LANES)
            span = pl.ds(head, count)
            for k in range(slots):
                image = lax.dot_general(
                    pairs[k][0], k_buf[0, k, lanes], contract, preferred_element_type=F32
                ) + lax.dot_general(
                    pairs[k][1], k_buf[1, k, lanes], contract, preferred_element_type=F32
                )
                for c in range(2):
                    for l in range(count):
                        img_send[
                            sweep,
                            head + l,
                            pl.ds(c * slots + k, n_param, stride=comps),
                            :,
                        ] = image[
                            c * n_param : (c + 1) * n_param,
                            l * LANES : (l + 1) * LANES,
                        ]

            def part(peer):
                start = pl.multiple_of(peer * comps, comps)
                return img_send.at[sweep, span, pl.ds(start, comps), :]

            arrive, left = exchange(
                "param",
                me_p,
                n_param,
                part,
                lambda slot: img_buf.at[sweep, slot, span],
                img_sems.at[sweep, i],
            )
            waits.append(arrive)
            pending.append(left)

        late = []
        own = pl.ds(pl.multiple_of(me_p * comps, comps), comps)
        for i, (head, count) in enumerate(chunks):
            span = pl.ds(head, count)
            img_buf[sweep, me_p, span] = img_send[sweep, span, own, :]
            waits[i]()
            total = img_buf[sweep, 0, span]
            for r in range(1, n_param):
                total = total + img_buf[sweep, r, span]
            row_send[sweep, span] = total
            arrive, left = exchange(
                "freq",
                me_f,
                n_freq,
                lambda peer: row_send.at[sweep, span],
                lambda slot: row_buf.at[sweep, slot, span],
                row_sems.at[sweep, i],
            )
            row_buf[sweep, me_f, span] = total
            late.append(arrive)
            pending.append(left)

        inverse = []
        for i, (head, count) in enumerate(chunks):
            late[i]()
            for l in range(head, head + count):
                inverse.append(
                    weighted(
                        inv_wide,
                        [
                            row_buf[sweep, j, l, c : c + 1, :]
                            for j in range(n_freq)
                            for c in range(comps)
                        ],
                    )
                )
        applied = noise * direction + jnp.concatenate(inverse, axis=1)
        step_len = norm_now / jnp.sum(direction * applied, keepdims=True)
        solution = solution + step_len * direction
        residual = residual - step_len * applied
        if sweep + 1 < ITERS:
            norm_next = jnp.sum(residual * residual, keepdims=True)
            direction = residual + (norm_next / norm_now) * direction
            norm_now = norm_next

    for out_ref, value in ((sol_ref, solution), (res_ref, residual)):
        own = value[:block]
        for j in range(1, n_freq):
            own = jnp.where(me_f == j, value[j * block : (j + 1) * block], own)
        out_ref[...] = own[:, :sensors]
    for left in pending:
        left()


def solution(mesh):
    n_param, n_freq = mesh.shape["param"], mesh.shape["freq"]

    def local(kernel_hat, prior_gain, noise_var, observed):
        _, slots, sensors, params = kernel_hat.shape
        rows, block, _ = observed.shape
        assert rows == 1
        times = block * n_freq
        padded = -(-sensors // LANES) * LANES
        tiles = padded // LANES
        parts = len(sensor_chunks(padded))
        comps = 2 * slots
        cos, sin = phase_tables(slots * n_freq, times)
        pieces = np.stack([cos, -sin]).reshape(2, n_freq, slots, times)
        forward = pieces.transpose(1, 0, 2, 3).reshape(n_freq, comps, times)
        inverse = forward.reshape(n_freq * comps, times).T.copy()
        vmem = pl.BlockSpec(memory_space=pltpu.VMEM)
        out = jax.ShapeDtypeStruct((block, sensors), F32)
        dma = pltpu.SemaphoreType.DMA
        results = pl.pallas_call(
            functools.partial(kernel, n_param, n_freq),
            out_shape=(out, out),
            in_specs=[pl.BlockSpec(memory_space=pltpu.HBM)] * 6,
            out_specs=(vmem, vmem),
            scratch_shapes=[
                pltpu.VMEM((2, slots, padded, params), BF16),
                pltpu.VMEM((n_freq, block, sensors), F32),
                pltpu.VMEM((slots, params), F32),
                pltpu.VMEM((sensors,), F32),
                pltpu.VMEM((comps, times), F32),
                pltpu.VMEM(inverse.shape, F32),
                pltpu.VMEM((times, comps, LANES), F32),
                pltpu.VMEM((comps * n_freq, times, LANES), F32),
                pltpu.VMEM((ITERS, comps, padded), BF16),
                pltpu.VMEM((ITERS, n_param, comps, padded), BF16),
                pltpu.VMEM((tiles, n_param * comps, LANES), F32),
                pltpu.VMEM((ITERS, tiles, n_param * comps, LANES), F32),
                pltpu.VMEM((ITERS, n_param, tiles, comps, LANES), F32),
                pltpu.VMEM((ITERS, tiles, comps, LANES), F32),
                pltpu.VMEM((ITERS, n_freq, tiles, comps, LANES), F32),
                dma((parts,)),
                dma((5,)),
                dma((2, n_freq)),
                dma((ITERS, parts, 2, n_param)),
                dma((ITERS, parts, 2, n_param)),
                dma((ITERS, parts, 2, n_freq)),
            ],
            compiler_params=pltpu.CompilerParams(
                collective_id=0,
                has_side_effects=True,
            ),
        )(
            observed,
            kernel_hat,
            prior_gain,
            noise_var,
            jnp.asarray(forward),
            jnp.asarray(inverse),
        )
        return tuple(value.reshape(observed.shape) for value in results)

    return jax.shard_map(
        local,
        mesh=mesh,
        in_specs=(
            P(None, "freq", None, "param"),
            P("freq", "param"),
            P(),
            P("param", "freq", None),
        ),
        out_specs=(P("param", "freq", None), P("param", "freq", None)),
        check_vma=False,
    )
```

time: 51.3 us -> 46.8 us (0.912)
  Pallas kernels: 45.5 us -> 43.2 us
  local copies, waits for them, and re-layouts: 4.72 us -> 2.6 us
    pallas_call x1, Pallas kernels: 45.5 us -> 43.2 us  [local(): pl.pallas_call(functools.partial(kernel, n_param, n_freq), out_shape=(out...]
    unnamed x10 -> x2, local copies, waits for them, and re-layouts: 4.03 us -> 2.6 us
    reshape x1 -> x0, local copies, waits for them, and re-layouts: 0.69 us -> none  [local(): noise_var.reshape(1, sensors)]
where the time goes in v2:
time: 46.8 us; the launch traced here: 46.5 us
  Pallas kernels  43.2 us (92%)
  local copies, waits for them, and re-layouts  2.6 us (6%)
  between operations  0.64 us (1%)
    pallas_call x1, Pallas kernels, local(): pl.pallas_call(functools.partial(kernel, n_param, n_freq), out_shape=(out...  43.2 us
    unnamed x2, local copies, waits for them, and re-layouts  2.6 us

profile of v2, /device:TPU:0, one launch (start us, length us, event | category | flops | bytes accessed | tf_op | source)
XLA Modules:
  0.0 46.5 jit_solution(14516041022841419987)
XLA Ops:
  0.6 43.2 %shard_map.77 = (f32[4,600]{1,0:T(4,128)}, f32[4,600]{1,0:T(4,128)}) custom-call(f32[1,4,600]{2,1,0:T(4,128)} %obs_ref.1, bf16[2,4,600,1024]{3,2,1,0:T(8,128)(2,1)} %kernel_ref.1, f32[4,1024]{1,0:T(4,128)} %gain_ref.1, f32[600]{0:T(1024)} %noise_ref.1, f32[4,8,16]{2,1,0:T(8,128)} %constant.4.clone.fwd_ref, f32[16,32]{1,0:T(8,128)} %constant.5.clone.inv_ref), custom_call_target="tpu_custom_call" | custom-call | tf_op jit(solution)/shard_map/pallas_call | solution.py:356
  43.9 1.3 %copy.10 = f32[1,4,600]{2,1,0:T(4,128)} copy(f32[1,4,600]{2,1,0:T(4,128)} %bitcast.3) | data formatting | bytes 19200
  45.2 1.3 %copy.11 = f32[1,4,600]{2,1,0:T(4,128)} copy(f32[1,4,600]{2,1,0:T(4,128)} %bitcast.2) | data formatting | bytes 19200
